TPU v7x, 32 devices: a whole 2x2x4 slice. The times are simulated.
32 devices in a mesh: row: 4 (over y, x), col: 8 (over z, core).
Axes of the slice: x: 2, y: 2, z: 4, core: 2. Of those that a mesh axis runs over, the one named last changes fastest.
Arguments:
- initial_field: float32 [1, 512, 4096], P(None, 'row', 'col'), may hold values from -12 to 12
- information: float32 [512, 4096], P('row', 'col'), may hold values from -24 to 24
- kappa_squared: float32 [512, 4096], P('row', 'col'), may hold values from 0.05 to 2
- lumped_mass: float32 [512, 4096], P('row', 'col'), may hold values from 0.5 to 2
- noise_seeds: int32 [4, 8, 2, 4, 1], P('row', 'col'), may hold values from 0 to 1073741823
- colour_order: int32 [4], replicated, may hold values from 0 to 3, each once
Outputs:
- final_field: float32 [1, 512, 4096], P(None, 'row', 'col')
- energies: float32 [2, 4, 1], replicated
Inputs may be any that keep to these rules, and one draw needn't show every extreme that they name: `noise_seeds`: one seed for each tile of 128 x 512 nodes, sweep, colour phase and chain. `colour_order`: names each of the 4 block colours once.
All inputs are finite; a program needn't handle non-finite values.
Results may differ from a plain program's by a relative error of at most 0.0003.
Values sent between devices are 32-bit elements; how exact they have to be, the bound alone decides.
No kernel may reach another device: no remote copies, remote signals or barrier semaphores. Data moves between devices by JAX's collectives and lax.ppermute only.
A program may use at most 128 MiB of HBM per device.

v0:
```python
import jax
import jax.numpy as jnp
from jax import lax
from jax.sharding import PartitionSpec as P

SWEEPS = 2
COLOURS = 4
full_turn = 6.283185307179586
unit_step = 1.0 / 8388608.0
mix_factor = 73244475


def with_halo(block, sides, width):
    for axis, dim in sides:
        count = lax.axis_size(axis)
        forward = [(i, i + 1) for i in range(count - 1)]
        forward.append((count - 1, 0))
        backward = [(target, source) for source, target in forward]
        low = lax.ppermute(
            lax.slice_in_dim(block, block.shape[dim] - width, None, axis=dim), axis, forward
        )
        high = lax.ppermute(lax.slice_in_dim(block, 0, width, axis=dim), axis, backward)
        block = jnp.concatenate([low, block, high], axis=dim)
    return block


def crop_edges(source, amount):
    return source[..., amount : source.shape[-2] - amount, amount : source.shape[-1] - amount]


def stencil_sum(source):
    return (
        source[..., :-2, 1:-1]
        + source[..., 2:, 1:-1]
        + source[..., 1:-1, :-2]
        + source[..., 1:-1, 2:]
    )


def apply_precision(sample_field, stiffness, inverse):
    first_pass = stiffness * crop_edges(sample_field, 1) - stencil_sum(sample_field)
    scaled = inverse * first_pass
    return crop_edges(stiffness, 1) * crop_edges(scaled, 1) - stencil_sum(scaled)


def corners(source):
    return [
        source[..., first_index::2, second_index::2]
        for first_index in (0, 1)
        for second_index in (0, 1)
    ]


def join_corners(pieces):
    total = None
    for corner in range(4):
        piece = pieces[corner]
        row_parity, col_parity = (corner // 2, corner % 2)
        config = [(0, 0, 0)] * (piece.ndim - 2) + [
            (row_parity, 1 - row_parity, 1),
            (col_parity, 1 - col_parity, 1),
        ]
        padded = lax.pad(piece, jnp.zeros((), piece.dtype), config)
        total = padded if total is None else total + padded
    return total


def block_matrix(stiff_corners, inverse_corners, diagonal_corners):
    scaled = [stiff_corners[corner] * inverse_corners[corner] for corner in range(4)]
    matrix = [[None] * 4 for corner in range(4)]
    for corner in range(4):
        matrix[corner][corner] = diagonal_corners[corner]
    for first_index, second_index in ((0, 1), (0, 2), (1, 3), (2, 3)):
        element = -(scaled[first_index] + scaled[second_index])
        matrix[first_index][second_index] = element
        matrix[second_index][first_index] = element
    matrix[0][3] = inverse_corners[1] + inverse_corners[2]
    matrix[3][0] = matrix[0][3]
    matrix[1][2] = inverse_corners[0] + inverse_corners[3]
    matrix[2][1] = matrix[1][2]
    return matrix


def cholesky_rows(matrix):
    factor = [[None] * 4 for corner in range(4)]
    for first_index in range(4):
        for second_index in range(first_index + 1):
            running = matrix[first_index][second_index]
            for middle in range(second_index):
                running = running - factor[first_index][middle] * factor[second_index][middle]
            if first_index == second_index:
                factor[first_index][first_index] = jnp.sqrt(running)
            else:
                factor[first_index][second_index] = running / factor[second_index][second_index]
    return factor


def crop_matrix(matrix, amount):
    return [
        [None if element is None else crop_edges(element, amount) for element in matrix_row]
        for matrix_row in matrix
    ]


def resample(field_corners, applied_corners, info_corners, matrix, factor, noise_list):
    right_side = []
    for first_index in range(4):
        coupled = matrix[first_index][0] * field_corners[0]
        for second_index in range(1, 4):
            coupled = coupled + matrix[first_index][second_index] * field_corners[second_index]
        right_side.append(info_corners[first_index] - applied_corners[first_index] + coupled)
    forward = []
    for first_index in range(4):
        running = right_side[first_index]
        for second_index in range(first_index):
            running = running - factor[first_index][second_index] * forward[second_index]
        forward.append(running / factor[first_index][first_index])
    shifted = [forward[corner] + noise_list[corner] for corner in range(4)]
    result = [None] * 4
    for first_index in reversed(range(4)):
        running = shifted[first_index]
        for second_index in range(first_index + 1, 4):
            running = running - factor[second_index][first_index] * result[second_index]
        result[first_index] = running / factor[first_index][first_index]
    return result


def scramble(hashed):
    sixteen = jnp.full_like(hashed, 16)
    hashed = hashed ^ lax.shift_right_logical(hashed, sixteen)
    hashed = hashed * mix_factor
    hashed = hashed ^ lax.shift_right_logical(hashed, sixteen)
    hashed = hashed * mix_factor
    return hashed ^ lax.shift_right_logical(hashed, sixteen)


def gaussian(seed_nodes, offsets):
    first_hash = scramble(seed_nodes + 2 * offsets)
    second_hash = scramble(seed_nodes + 2 * offsets + 1)
    shift_nine = jnp.full_like(first_hash, 9)
    uniform_one = (
        lax.shift_right_logical(first_hash, shift_nine).astype(jnp.float32) + 1.0
    ) * unit_step
    uniform_two = lax.shift_right_logical(second_hash, shift_nine).astype(jnp.float32) * unit_step
    return jnp.sqrt(-2.0 * jnp.log(uniform_one)) * jnp.cos(full_turn * uniform_two)


def node_seeds(seed_table, which_rows, which_cols):
    result = jnp.zeros((seed_table.shape[-1], which_rows.shape[0], which_cols.shape[0]), jnp.int32)
    hit = (which_rows == 0)[:, None] & (which_cols == 0)[None, :]
    result = result + jnp.where(hit[None], seed_table[0, 0][:, None, None], 0)
    return result


def local(initial_field, information, kappa_squared, lumped_mass, noise_seeds, colour_order):
    chains, tile_rows, tile_cols = initial_field.shape
    total_rows = tile_rows * lax.axis_size("row")
    total_cols = tile_cols * lax.axis_size("col")
    row_start = lax.axis_index("row") * tile_rows
    col_start = lax.axis_index("col") * tile_cols
    kappa_ext, mass_ext = (
        with_halo(kappa_squared, (("row", 0), ("col", 1)), 1),
        with_halo(lumped_mass, (("row", 0), ("col", 1)), 1),
    )
    margin = 2
    info_margin = (information.shape[0] - tile_rows) // 2
    stiff_ext = kappa_ext * mass_ext + 4.0
    inverse_ext = 1.0 / mass_ext
    block_margin = margin - 2
    stiff_blocks = crop_edges(stiff_ext, 1)
    inverse_blocks = crop_edges(inverse_ext, 1)
    diagonal = stiff_blocks * stiff_blocks * inverse_blocks + stencil_sum(inverse_ext)
    matrix = block_matrix(corners(stiff_blocks), corners(inverse_blocks), corners(diagonal))
    factor = cholesky_rows(matrix)
    shrink_table = 1 - noise_seeds.shape[0] // 2

    def phase_tables(near_margin):
        half_rows = jnp.arange((tile_rows + 2 * near_margin) // 2, dtype=jnp.int32)
        half_cols = jnp.arange((tile_cols + 2 * near_margin) // 2, dtype=jnp.int32)
        block_rows = (row_start - near_margin) // 2 + half_rows
        block_cols = (col_start - near_margin) // 2 + half_cols
        block_colour = 2 * (block_rows % 2)[:, None] + (block_cols % 2)[None, :]
        offsets = []
        row_tiles = []
        col_tiles = []
        for corner in range(4):
            local_rows = 2 * half_rows + corner // 2 - near_margin
            local_cols = 2 * half_cols + corner % 2 - near_margin
            global_rows = (row_start + local_rows) % total_rows
            global_cols = (col_start + local_cols) % total_cols
            offsets.append(
                (global_rows % tile_rows)[:, None] * tile_cols + (global_cols % tile_cols)[None, :]
            )
            row_tiles.append(
                (local_rows >= 0).astype(jnp.int32)
                + (local_rows >= tile_rows).astype(jnp.int32)
                - shrink_table
            )
            col_tiles.append(
                (local_cols >= 0).astype(jnp.int32)
                + (local_cols >= tile_cols).astype(jnp.int32)
                - shrink_table
            )
        return (block_colour, offsets, row_tiles, col_tiles)

    def one_sweep(sweep_index, loop_state):
        sample_field, energies = loop_state
        seed_layer = lax.dynamic_index_in_dim(noise_seeds, sweep_index, 2, keepdims=False)
        for phase_index in range(COLOURS):
            extended = with_halo(sample_field, (("row", 1), ("col", 2)), 2)
            margin_now = (extended.shape[1] - tile_rows) // 2
            near_margin = margin_now - 2
            applied = apply_precision(
                extended,
                crop_edges(stiff_ext, margin - margin_now),
                crop_edges(inverse_ext, margin - margin_now),
            )
            inner_field = crop_edges(extended, margin_now)
            inner_applied = crop_edges(applied, near_margin)
            local_energy = jnp.sum(
                0.5 * inner_field * inner_applied - information * inner_field, axis=(1, 2)
            )
            energies = energies.at[sweep_index, phase_index].set(local_energy)
            dropped = (block_margin - near_margin) // 2
            block_colour, offsets, row_tiles, col_tiles = phase_tables(near_margin)
            chosen = block_colour == colour_order[phase_index]
            near_field = crop_edges(extended, 2)
            near_info = crop_edges(information, info_margin - near_margin)
            seed_table = seed_layer[:, :, phase_index, :]
            noise_list = []
            for corner in range(4):
                seeds_here = node_seeds(seed_table, row_tiles[corner], col_tiles[corner])
                noise_list.append(gaussian(seeds_here, offsets[corner]))
            before = corners(near_field)
            updated = resample(
                before,
                corners(applied),
                corners(near_info),
                crop_matrix(matrix, dropped),
                crop_matrix(factor, dropped),
                noise_list,
            )
            extended = join_corners(
                [jnp.where(chosen, updated[corner], before[corner]) for corner in range(4)]
            )
            sample_field = extended
        return (sample_field, energies)

    initial = (initial_field, jnp.zeros((SWEEPS, COLOURS, chains), jnp.float32))
    final_field, energies = lax.fori_loop(0, SWEEPS, one_sweep, initial)
    energies = lax.psum(energies, ("row", "col")) / (total_rows * total_cols)
    return (final_field, energies)


def solution(mesh):
    placed = (
        P(None, "row", "col"),
        P("row", "col"),
        P("row", "col"),
        P("row", "col"),
        P("row", "col", None, None, None),
        P(),
    )
    return jax.shard_map(
        local, mesh=mesh, in_specs=placed, out_specs=(P(None, "row", "col"), P()), check_vma=False
    )
```

profile of v0, /device:TPU:0, one launch (start us, length us, event | category | flops | bytes accessed | tf_op | source)
XLA Modules:
  0.0 570.5 jit_solution(7635717978839268749)
XLA Ops:
  8.7 3.5 collective-permute-start.19
  12.4 3.5 collective-permute-start.23
  30.0 12.0 %slice.1365 = f32[64,256]{1,0:T(8,128)S(1)} slice(f32[128,512]{1,0:T(8,128)S(1)} %get-tuple-element.1169), slice={[0:128:2], [1:512:2]} | slice | bytes 131072 | tf_op jit(solution)/shard_map/slice | solution.py:48
  56.6 474.0 %while.22 = (s32[]{:T(128)}, f32[1,128,512]{2,1,0:T(8,128)S(1)}, f32[2,4,1]{1,2,0:T(1,128)}, s32[]{:T(128)}, s32[]{:T(128)}, /*index=5*/s32[4]{0:T(128)S(1)}, f3...) while((s32[]{:T(128)}, f32[1,128,512]{2,1,0:T(8,128)S(1)}, ...), condition=%wide.region_9.10_spmd, body=%wide.region_0.9_spmd.sunk | while | flops 21103232 | bytes 64269184 | solution.py:250
  108.1 3.6 pad.730
  111.7 3.6 pad.731
  148.9 3.3 fusion.562
  157.7 3.6 pad.733
  161.3 3.6 pad.734
  164.9 3.6 pad.735
  202.7 3.2 fusion.567
  208.2 4.5 pad.736
  212.7 3.6 pad.737
  216.3 3.6 pad.738
  219.9 3.7 pad.739
  283.2 3.6 pad.743
  344.5 3.6 pad.730
  348.1 3.6 pad.731
  380.9 3.2 slice.1689
  385.4 3.3 fusion.562
  394.2 3.6 pad.733
  397.8 3.6 pad.734
  401.4 3.6 pad.735
  433.8 3.2 slice.1697
  438.4 3.2 fusion.567
  444.0 4.5 pad.736
  448.4 3.6 pad.737
  452.0 3.6 pad.738
  455.7 3.7 pad.739
  493.9 3.2 slice.1704
  518.6 3.6 pad.743
  531.4 38.3 %psum.7 = f32[2,4,1]{1,2,0:T(1,128)S(1)} all-reduce(f32[2,4,1]{1,2,0:T(1,128)S(1)} %copy-done.55), channel_id=1, replica_groups=mesh['row'=4,'col'=8] {'row','col'}, use_global_device_ids=true, to_apply=%region_10.11 | all-reduce | flops 8 | bytes 64 | tf_op jit(solution)/shard_map/psum | solution.py:251
  (498 shorter events, 411.8 us)
Async XLA Ops:
  1.6 7.0 %collective-permute-start.16 = (f32[1,512]{1,0:T(1,128)S(1)}, f32[1,512]{1,0:T(1,128)S(1)}, u32[]{:S(2)}, u32[]{:S(2)}) collective-permute-start(f32[1,512]{1,0:T(1,128)S(1)} %get-tuple-element.1176), channel_id=1, source_target_pairs={{0,8},{8,16},{16,24},{24,0},{1,9},{9,17},{17,25},{25,1},{2,10},{10... | collective-permute-start | bytes 6152 | tf_op jit(solution)/shard_map/ppermute | solution.py:19
  5.6 6.7 %collective-permute-start.20 = (f32[1,512]{1,0:T(1,128)S(1)}, f32[1,512]{1,0:T(1,128)S(1)}, u32[]{:S(2)}, u32[]{:S(2)}) collective-permute-start(f32[1,512]{1,0:T(1,128)S(1)} %get-tuple-element.1174), channel_id=1, source_target_pairs={{0,8},{8,16},{16,24},{24,0},{1,9},{9,17},{17,25},{25,1},{2,10},{10... | collective-permute-start | bytes 6152 | tf_op jit(solution)/shard_map/ppermute | solution.py:19
  6.6 5.6 collective-permute-start.21
  8.6 7.3 %collective-permute-start.18 = (f32[130,1]{1,0:T(8,128)S(1)}, f32[130,1]{1,0:T(8,128)S(1)}, u32[]{:S(2)}, u32[]{:S(2)}) collective-permute-start(f32[130,1]{1,0:T(8,128)S(1)} %get-tuple-element.1172), channel_id=1, source_target_pairs={{0,1},{1,2},{2,3},{3,4},{4,5},{5,6},{6,7},{7,0},{8,9},{9,10},{10,1... | collective-permute-start | bytes 1568 | tf_op jit(solution)/shard_map/ppermute | solution.py:19
  8.7 7.2 %collective-permute-start.19 = (f32[130,1]{1,0:T(8,128)S(1)}, f32[130,1]{1,0:T(8,128)S(1)}, u32[]{:S(2)}, u32[]{:S(2)}) collective-permute-start(f32[130,1]{1,0:T(8,128)S(1)} %get-tuple-element.1173), channel_id=1, source_target_pairs={{1,0},{2,1},{3,2},{4,3},{5,4},{6,5},{7,6},{0,7},{9,8},{10,9},{11,1... | collective-permute-start | bytes 1568 | tf_op jit(solution)/shard_map/ppermute | solution.py:22
  12.3 5.7 collective-permute-start.22
  12.4 5.6 collective-permute-start.23
  56.7 4.2 collective-permute-start
  58.3 4.5 collective-permute-start.1
  62.9 22.7 %collective-permute-start.2 = (f32[1,132,2]{2,1,0:T(8,128)S(1)}, f32[1,132,2]{2,1,0:T(8,128)S(1)}, u32[]{:S(2)}, u32[]{:S(2)}) collective-permute-start(f32[1,132,2]{2,1,0:T(8,128)S(1)} %get-tuple-element.1460), channel_id=1, source_target_pairs={{1,0},{2,1},{3,2},{4,3},{5,4},{6,5},{7,6},{0,7},{9,8},{10,9},{11,1... | collective-permute-start | bytes 3176 | tf_op jit(solution)/shard_map/while/body/eval_jaxpr/ppermute | solution.py:22
  64.9 20.6 %collective-permute-start.3 = (f32[1,132,2]{2,1,0:T(8,128)S(1)}, f32[1,132,2]{2,1,0:T(8,128)S(1)}, u32[]{:S(2)}, u32[]{:S(2)}) collective-permute-start(f32[1,132,2]{2,1,0:T(8,128)S(1)} %get-tuple-element.1461), channel_id=1, source_target_pairs={{0,1},{1,2},{2,3},{3,4},{4,5},{5,6},{6,7},{7,0},{8,9},{9,10},{10,1... | collective-permute-start | bytes 3176 | tf_op jit(solution)/shard_map/while/body/eval_jaxpr/ppermute | solution.py:19
  117.9 4.5 collective-permute-start.5
  122.5 13.1 %collective-permute-start.6 = (f32[1,132,2]{2,1,0:T(8,128)S(1)}, f32[1,132,2]{2,1,0:T(8,128)S(1)}, u32[]{:S(2)}, u32[]{:S(2)}) collective-permute-start(f32[1,132,2]{2,1,0:T(8,128)S(1)} %get-tuple-element.1483), channel_id=1, source_target_pairs={{1,0},{2,1},{3,2},{4,3},{5,4},{6,5},{7,6},{0,7},{9,8},{10,9},{11,1... | collective-permute-start | bytes 3176 | tf_op jit(solution)/shard_map/while/body/eval_jaxpr/ppermute | solution.py:22
  124.6 10.9 %collective-permute-start.7 = (f32[1,132,2]{2,1,0:T(8,128)S(1)}, f32[1,132,2]{2,1,0:T(8,128)S(1)}, u32[]{:S(2)}, u32[]{:S(2)}) collective-permute-start(f32[1,132,2]{2,1,0:T(8,128)S(1)} %get-tuple-element.1484), channel_id=1, source_target_pairs={{0,1},{1,2},{2,3},{3,4},{4,5},{5,6},{6,7},{7,0},{8,9},{9,10},{10,1... | collective-permute-start | bytes 3176 | tf_op jit(solution)/shard_map/while/body/eval_jaxpr/ppermute | solution.py:19
  170.9 4.5 collective-permute-start.9
  176.1 12.7 %collective-permute-start.10 = (f32[1,132,2]{2,1,0:T(8,128)}, f32[1,132,2]{2,1,0:T(8,128)S(1)}, u32[]{:S(2)}, u32[]{:S(2)}) collective-permute-start(f32[1,132,2]{2,1,0:T(8,128)} %get-tuple-element.1499), channel_id=1, source_target_pairs={{1,0},{2,1},{3,2},{4,3},{5,4},{6,5},{7,6},{0,7},{9,8},{10,9},{11,1... | collective-permute-start | bytes 3176 | tf_op jit(solution)/shard_map/while/body/eval_jaxpr/ppermute | solution.py:22
  178.2 10.6 %collective-permute-start.11 = (f32[1,132,2]{2,1,0:T(8,128)S(1)}, f32[1,132,2]{2,1,0:T(8,128)S(1)}, u32[]{:S(2)}, u32[]{:S(2)}) collective-permute-start(f32[1,132,2]{2,1,0:T(8,128)S(1)} %get-tuple-element.1500), channel_id=1, source_target_pairs={{0,1},{1,2},{2,3},{3,4},{4,5},{5,6},{6,7},{7,0},{8,9},{9,10},{10,1... | collective-permute-start | bytes 3176 | tf_op jit(solution)/shard_map/while/body/eval_jaxpr/ppermute | solution.py:19
  226.3 4.5 collective-permute-start.13
  231.5 15.4 %collective-permute-start.14 = (f32[1,132,2]{2,1,0:T(8,128)}, f32[1,132,2]{2,1,0:T(8,128)}, u32[]{:S(2)}, u32[]{:S(2)}) collective-permute-start(f32[1,132,2]{2,1,0:T(8,128)} %get-tuple-element.1515), channel_id=1, source_target_pairs={{1,0},{2,1},{3,2},{4,3},{5,4},{6,5},{7,6},{0,7},{9,8},{10,9},{11,1... | collective-permute-start | bytes 3176 | tf_op jit(solution)/shard_map/while/body/eval_jaxpr/ppermute | solution.py:22
  233.6 13.3 %collective-permute-start.15 = (f32[1,132,2]{2,1,0:T(8,128)}, f32[1,132,2]{2,1,0:T(8,128)}, u32[]{:S(2)}, u32[]{:S(2)}) collective-permute-start(f32[1,132,2]{2,1,0:T(8,128)} %get-tuple-element.1516), channel_id=1, source_target_pairs={{0,1},{1,2},{2,3},{3,4},{4,5},{5,6},{6,7},{7,0},{8,9},{9,10},{10,1... | collective-permute-start | bytes 3176 | tf_op jit(solution)/shard_map/while/body/eval_jaxpr/ppermute | solution.py:19
  294.5 4.5 collective-permute-start.1
  299.1 23.1 %collective-permute-start.2 = (f32[1,132,2]{2,1,0:T(8,128)S(1)}, f32[1,132,2]{2,1,0:T(8,128)S(1)}, u32[]{:S(2)}, u32[]{:S(2)}) collective-permute-start(f32[1,132,2]{2,1,0:T(8,128)S(1)} %get-tuple-element.1460), channel_id=1, source_target_pairs={{1,0},{2,1},{3,2},{4,3},{5,4},{6,5},{7,6},{0,7},{9,8},{10,9},{11,1... | collective-permute-start | bytes 3176 | tf_op jit(solution)/shard_map/while/body/eval_jaxpr/ppermute | solution.py:22
  301.4 20.8 %collective-permute-start.3 = (f32[1,132,2]{2,1,0:T(8,128)S(1)}, f32[1,132,2]{2,1,0:T(8,128)S(1)}, u32[]{:S(2)}, u32[]{:S(2)}) collective-permute-start(f32[1,132,2]{2,1,0:T(8,128)S(1)} %get-tuple-element.1461), channel_id=1, source_target_pairs={{0,1},{1,2},{2,3},{3,4},{4,5},{5,6},{6,7},{7,0},{8,9},{9,10},{10,1... | collective-permute-start | bytes 3176 | tf_op jit(solution)/shard_map/while/body/eval_jaxpr/ppermute | solution.py:19
  354.1 4.5 collective-permute-start.5
  358.7 13.1 %collective-permute-start.6 = (f32[1,132,2]{2,1,0:T(8,128)S(1)}, f32[1,132,2]{2,1,0:T(8,128)S(1)}, u32[]{:S(2)}, u32[]{:S(2)}) collective-permute-start(f32[1,132,2]{2,1,0:T(8,128)S(1)} %get-tuple-element.1483), channel_id=1, source_target_pairs={{1,0},{2,1},{3,2},{4,3},{5,4},{6,5},{7,6},{0,7},{9,8},{10,9},{11,1... | collective-permute-start | bytes 3176 | tf_op jit(solution)/shard_map/while/body/eval_jaxpr/ppermute | solution.py:22
  360.9 11.0 %collective-permute-start.7 = (f32[1,132,2]{2,1,0:T(8,128)S(1)}, f32[1,132,2]{2,1,0:T(8,128)S(1)}, u32[]{:S(2)}, u32[]{:S(2)}) collective-permute-start(f32[1,132,2]{2,1,0:T(8,128)S(1)} %get-tuple-element.1484), channel_id=1, source_target_pairs={{0,1},{1,2},{2,3},{3,4},{4,5},{5,6},{6,7},{7,0},{8,9},{9,10},{10,1... | collective-permute-start | bytes 3176 | tf_op jit(solution)/shard_map/while/body/eval_jaxpr/ppermute | solution.py:19
  406.6 4.5 collective-permute-start.9
  411.7 12.5 %collective-permute-start.10 = (f32[1,132,2]{2,1,0:T(8,128)}, f32[1,132,2]{2,1,0:T(8,128)S(1)}, u32[]{:S(2)}, u32[]{:S(2)}) collective-permute-start(f32[1,132,2]{2,1,0:T(8,128)} %get-tuple-element.1499), channel_id=1, source_target_pairs={{1,0},{2,1},{3,2},{4,3},{5,4},{6,5},{7,6},{0,7},{9,8},{10,9},{11,1... | collective-permute-start | bytes 3176 | tf_op jit(solution)/shard_map/while/body/eval_jaxpr/ppermute | solution.py:22
  413.9 10.3 %collective-permute-start.11 = (f32[1,132,2]{2,1,0:T(8,128)S(1)}, f32[1,132,2]{2,1,0:T(8,128)S(1)}, u32[]{:S(2)}, u32[]{:S(2)}) collective-permute-start(f32[1,132,2]{2,1,0:T(8,128)S(1)} %get-tuple-element.1500), channel_id=1, source_target_pairs={{0,1},{1,2},{2,3},{3,4},{4,5},{5,6},{6,7},{7,0},{8,9},{9,10},{10,1... | collective-permute-start | bytes 3176 | tf_op jit(solution)/shard_map/while/body/eval_jaxpr/ppermute | solution.py:19
  461.7 4.5 collective-permute-start.13
  466.9 15.2 %collective-permute-start.14 = (f32[1,132,2]{2,1,0:T(8,128)}, f32[1,132,2]{2,1,0:T(8,128)}, u32[]{:S(2)}, u32[]{:S(2)}) collective-permute-start(f32[1,132,2]{2,1,0:T(8,128)} %get-tuple-element.1515), channel_id=1, source_target_pairs={{1,0},{2,1},{3,2},{4,3},{5,4},{6,5},{7,6},{0,7},{9,8},{10,9},{11,1... | collective-permute-start | bytes 3176 | tf_op jit(solution)/shard_map/while/body/eval_jaxpr/ppermute | solution.py:22
  469.0 13.1 %collective-permute-start.15 = (f32[1,132,2]{2,1,0:T(8,128)}, f32[1,132,2]{2,1,0:T(8,128)}, u32[]{:S(2)}, u32[]{:S(2)}) collective-permute-start(f32[1,132,2]{2,1,0:T(8,128)} %get-tuple-element.1516), channel_id=1, source_target_pairs={{0,1},{1,2},{2,3},{3,4},{4,5},{5,6},{6,7},{7,0},{8,9},{9,10},{10,1... | collective-permute-start | bytes 3176 | tf_op jit(solution)/shard_map/while/body/eval_jaxpr/ppermute | solution.py:19
  (115 other events, 2332.5 us)
where the time goes:
time: 582 us; the launch traced here: 570 us
  local copies, waits for them, and re-layouts  356 us (61%)
  other arithmetic  95.8 us (16%)
  starting transfers between devices  49.4 us (8%)
  blocking collectives  38.3 us (7%)
  waiting for transfers between devices  26.1 us (4%)
    slice x84, local copies, waits for them, and re-layouts, corners(): source[..., first_index::2, second_index::2]  233 us
    pad x32, local copies, waits for them, and re-layouts, join_corners(): padded = lax.pad(piece, jnp.zeros((), piece.dtype), config)  103 us
    select_n x16, other arithmetic, one_sweep(): jnp.where(chosen, updated[corner], before[corner])  39.5 us
    psum x1, blocking collectives, local(): energies = lax.psum(energies, ('row', 'col')) / (total_rows * total_cols)  38.3 us
    ppermute x20, starting transfers between devices, with_halo(): lax.ppermute(lax.slice_in_dim(block, 0, width, axis=dim), axis, backward)  35.9 us
    ppermute x20, waiting for transfers between devices, with_halo(): lax.ppermute(lax.slice_in_dim(block, block.shape[dim] - width, None, axis...  16.6 us
    another operation x10, other arithmetic  16 us
    ppermute x20, starting transfers between devices, with_halo(): lax.ppermute(lax.slice_in_dim(block, block.shape[dim] - width, None, axis...  13.5 us
  transfers between devices with their start and end apart: 40, of which 15 were waited for; matrix products, arithmetic and copies ran while one was open for 20% of the time, Pallas kernels for 0%

commit v1 on v0

--- a/solution.py
+++ b/solution.py
@@ -248,7 +248,7 @@
 
     initial = (initial_field, jnp.zeros((SWEEPS, COLOURS, chains), jnp.float32))
     final_field, energies = lax.fori_loop(0, SWEEPS, one_sweep, initial)
-    energies = lax.psum(energies, ("row", "col")) / (total_rows * total_cols)
+    energies = lax.psum(lax.psum(energies, "col"), "row") / (total_rows * total_cols)
     return (final_field, energies)
 
 

time: 582 us -> 568 us (0.976)
  blocking collectives: 38.3 us -> 25 us
    psum x1 -> x2, blocking collectives: 38.3 us -> 25 us  [the longest x1 17.1 us: local(): lax.psum(energies, 'col')]
where the time goes in v1:
time: 568 us; the launch traced here: 557 us
  local copies, waits for them, and re-layouts  356 us (63%)
  other arithmetic  95.6 us (17%)
  starting transfers between devices  49.3 us (9%)
  waiting for transfers between devices  26.2 us (5%)
  blocking collectives  25 us (4%)
    slice x84, local copies, waits for them, and re-layouts, corners(): source[..., first_index::2, second_index::2]  233 us
    pad x32, local copies, waits for them, and re-layouts, join_corners(): padded = lax.pad(piece, jnp.zeros((), piece.dtype), config)  103 us
    select_n x16, other arithmetic, one_sweep(): jnp.where(chosen, updated[corner], before[corner])  39.1 us
    ppermute x20, starting transfers between devices, with_halo(): lax.ppermute(lax.slice_in_dim(block, 0, width, axis=dim), axis, backward)  35.9 us
    psum x1, blocking collectives, local(): lax.psum(energies, 'col')  17.1 us
    ppermute x20, waiting for transfers between devices, with_halo(): lax.ppermute(lax.slice_in_dim(block, block.shape[dim] - width, None, axis...  16.7 us
    another operation x10, other arithmetic  16.1 us
    ppermute x20, starting transfers between devices, with_halo(): lax.ppermute(lax.slice_in_dim(block, block.shape[dim] - width, None, axis...  13.5 us
  transfers between devices with their start and end apart: 40, of which 15 were waited for; matrix products, arithmetic and copies ran while one was open for 20% of the time, Pallas kernels for 0%

profile of v1, /device:TPU:0, one launch (start us, length us, event | category | flops | bytes accessed | tf_op | source)
XLA Modules:
  0.0 556.7 jit_solution(1745784795266793461)
XLA Ops:
  8.7 3.5 collective-permute-start.19
  12.4 3.5 collective-permute-start.23
  30.0 12.0 %slice.1365 = f32[64,256]{1,0:T(8,128)S(1)} slice(f32[128,512]{1,0:T(8,128)S(1)} %get-tuple-element.1169), slice={[0:128:2], [1:512:2]} | slice | bytes 131072 | tf_op jit(solution)/shard_map/slice | solution.py:48
  56.6 473.5 %while.22 = (s32[]{:T(128)}, f32[1,128,512]{2,1,0:T(8,128)S(1)}, f32[2,4,1]{1,2,0:T(1,128)}, s32[]{:T(128)}, s32[]{:T(128)}, /*index=5*/s32[4]{0:T(128)S(1)}, f3...) while((s32[]{:T(128)}, f32[1,128,512]{2,1,0:T(8,128)S(1)}, ...), condition=%wide.region_9.10_spmd, body=%wide.region_0.9_spmd.sunk | while | flops 21103232 | bytes 64269184 | solution.py:250
  108.0 3.6 pad.730
  111.6 3.6 pad.731
  157.4 3.6 pad.733
  161.0 3.6 pad.734
  164.6 3.6 pad.735
  202.5 3.3 fusion.567
  208.1 4.5 pad.736
  212.5 3.6 pad.737
  216.1 3.6 pad.738
  219.7 3.7 pad.739
  258.4 3.2 slice.1704
  283.1 3.6 pad.743
  344.3 3.6 pad.730
  347.9 3.6 pad.731
  380.7 3.2 slice.1689
  393.8 3.6 pad.733
  397.4 3.6 pad.734
  401.0 3.6 pad.735
  433.5 3.2 slice.1697
  438.1 3.3 fusion.567
  443.6 4.5 pad.736
  448.1 3.6 pad.737
  451.7 3.6 pad.738
  455.3 3.7 pad.739
  493.6 3.2 slice.1704
  518.4 3.6 pad.743
  530.9 17.1 %psum.14 = f32[2,4,1]{1,2,0:T(1,128)S(1)} all-reduce(f32[2,4,1]{1,2,0:T(1,128)S(1)} %copy-done.55), channel_id=1, replica_groups=mesh['row'=4,'col'=8] {'col'}, use_global_device_ids=true, to_apply=%region_10.11 | all-reduce | flops 8 | bytes 64 | tf_op jit(solution)/shard_map/psum | solution.py:251
  548.0 7.9 %psum.15 = f32[2,4,1]{1,2,0:T(1,128)S(1)} all-reduce(f32[2,4,1]{1,2,0:T(1,128)S(1)} %psum.14), channel_id=1, replica_groups=mesh['row'=4,'col'=8] {'row'}, use_global_device_ids=true, to_apply=%region_11.12 | all-reduce | flops 8 | bytes 64 | tf_op jit(solution)/shard_map/psum | solution.py:251
  (499 shorter events, 415.0 us)
Async XLA Ops:
  1.6 7.0 %collective-permute-start.16 = (f32[1,512]{1,0:T(1,128)S(1)}, f32[1,512]{1,0:T(1,128)S(1)}, u32[]{:S(2)}, u32[]{:S(2)}) collective-permute-start(f32[1,512]{1,0:T(1,128)S(1)} %get-tuple-element.1176), channel_id=1, source_target_pairs={{0,8},{8,16},{16,24},{24,0},{1,9},{9,17},{17,25},{25,1},{2,10},{10... | collective-permute-start | bytes 6152 | tf_op jit(solution)/shard_map/ppermute | solution.py:19
  5.6 6.7 %collective-permute-start.20 = (f32[1,512]{1,0:T(1,128)S(1)}, f32[1,512]{1,0:T(1,128)S(1)}, u32[]{:S(2)}, u32[]{:S(2)}) collective-permute-start(f32[1,512]{1,0:T(1,128)S(1)} %get-tuple-element.1174), channel_id=1, source_target_pairs={{0,8},{8,16},{16,24},{24,0},{1,9},{9,17},{17,25},{25,1},{2,10},{10... | collective-permute-start | bytes 6152 | tf_op jit(solution)/shard_map/ppermute | solution.py:19
  6.6 5.6 %collective-permute-start.21 = (f32[1,512]{1,0:T(1,128)S(1)}, f32[1,512]{1,0:T(1,128)S(1)}, u32[]{:S(2)}, u32[]{:S(2)}) collective-permute-start(f32[1,512]{1,0:T(1,128)S(1)} %get-tuple-element.1175), channel_id=1, source_target_pairs={{8,0},{16,8},{24,16},{0,24},{9,1},{17,9},{25,17},{1,25},{10,2},{18... | collective-permute-start | bytes 6152 | tf_op jit(solution)/shard_map/ppermute | solution.py:22
  8.6 7.3 %collective-permute-start.18 = (f32[130,1]{1,0:T(8,128)S(1)}, f32[130,1]{1,0:T(8,128)S(1)}, u32[]{:S(2)}, u32[]{:S(2)}) collective-permute-start(f32[130,1]{1,0:T(8,128)S(1)} %get-tuple-element.1172), channel_id=1, source_target_pairs={{0,1},{1,2},{2,3},{3,4},{4,5},{5,6},{6,7},{7,0},{8,9},{9,10},{10,1... | collective-permute-start | bytes 1568 | tf_op jit(solution)/shard_map/ppermute | solution.py:19
  8.7 7.2 %collective-permute-start.19 = (f32[130,1]{1,0:T(8,128)S(1)}, f32[130,1]{1,0:T(8,128)S(1)}, u32[]{:S(2)}, u32[]{:S(2)}) collective-permute-start(f32[130,1]{1,0:T(8,128)S(1)} %get-tuple-element.1173), channel_id=1, source_target_pairs={{1,0},{2,1},{3,2},{4,3},{5,4},{6,5},{7,6},{0,7},{9,8},{10,9},{11,1... | collective-permute-start | bytes 1568 | tf_op jit(solution)/shard_map/ppermute | solution.py:22
  12.3 5.7 %collective-permute-start.22 = (f32[130,1]{1,0:T(8,128)S(1)}, f32[130,1]{1,0:T(8,128)S(1)}, u32[]{:S(2)}, u32[]{:S(2)}) collective-permute-start(f32[130,1]{1,0:T(8,128)S(1)} %get-tuple-element.1170), channel_id=1, source_target_pairs={{0,1},{1,2},{2,3},{3,4},{4,5},{5,6},{6,7},{7,0},{8,9},{9,10},{10,1... | collective-permute-start | bytes 1568 | tf_op jit(solution)/shard_map/ppermute | solution.py:19
  12.4 5.6 %collective-permute-start.23 = (f32[130,1]{1,0:T(8,128)S(1)}, f32[130,1]{1,0:T(8,128)S(1)}, u32[]{:S(2)}, u32[]{:S(2)}) collective-permute-start(f32[130,1]{1,0:T(8,128)S(1)} %get-tuple-element.1171), channel_id=1, source_target_pairs={{1,0},{2,1},{3,2},{4,3},{5,4},{6,5},{7,6},{0,7},{9,8},{10,9},{11,1... | collective-permute-start | bytes 1568 | tf_op jit(solution)/shard_map/ppermute | solution.py:22
  56.7 4.1 collective-permute-start
  58.3 4.5 collective-permute-start.1
  62.9 22.6 %collective-permute-start.2 = (f32[1,132,2]{2,1,0:T(8,128)S(1)}, f32[1,132,2]{2,1,0:T(8,128)S(1)}, u32[]{:S(2)}, u32[]{:S(2)}) collective-permute-start(f32[1,132,2]{2,1,0:T(8,128)S(1)} %get-tuple-element.1460), channel_id=1, source_target_pairs={{1,0},{2,1},{3,2},{4,3},{5,4},{6,5},{7,6},{0,7},{9,8},{10,9},{11,1... | collective-permute-start | bytes 3176 | tf_op jit(solution)/shard_map/while/body/eval_jaxpr/ppermute | solution.py:22
  64.9 20.6 %collective-permute-start.3 = (f32[1,132,2]{2,1,0:T(8,128)S(1)}, f32[1,132,2]{2,1,0:T(8,128)S(1)}, u32[]{:S(2)}, u32[]{:S(2)}) collective-permute-start(f32[1,132,2]{2,1,0:T(8,128)S(1)} %get-tuple-element.1461), channel_id=1, source_target_pairs={{0,1},{1,2},{2,3},{3,4},{4,5},{5,6},{6,7},{7,0},{8,9},{9,10},{10,1... | collective-permute-start | bytes 3176 | tf_op jit(solution)/shard_map/while/body/eval_jaxpr/ppermute | solution.py:19
  117.8 4.5 collective-permute-start.5
  122.4 13.1 %collective-permute-start.6 = (f32[1,132,2]{2,1,0:T(8,128)S(1)}, f32[1,132,2]{2,1,0:T(8,128)S(1)}, u32[]{:S(2)}, u32[]{:S(2)}) collective-permute-start(f32[1,132,2]{2,1,0:T(8,128)S(1)} %get-tuple-element.1483), channel_id=1, source_target_pairs={{1,0},{2,1},{3,2},{4,3},{5,4},{6,5},{7,6},{0,7},{9,8},{10,9},{11,1... | collective-permute-start | bytes 3176 | tf_op jit(solution)/shard_map/while/body/eval_jaxpr/ppermute | solution.py:22
  124.6 11.0 %collective-permute-start.7 = (f32[1,132,2]{2,1,0:T(8,128)S(1)}, f32[1,132,2]{2,1,0:T(8,128)S(1)}, u32[]{:S(2)}, u32[]{:S(2)}) collective-permute-start(f32[1,132,2]{2,1,0:T(8,128)S(1)} %get-tuple-element.1484), channel_id=1, source_target_pairs={{0,1},{1,2},{2,3},{3,4},{4,5},{5,6},{6,7},{7,0},{8,9},{9,10},{10,1... | collective-permute-start | bytes 3176 | tf_op jit(solution)/shard_map/while/body/eval_jaxpr/ppermute | solution.py:19
  170.6 4.5 collective-permute-start.9
  175.8 12.7 %collective-permute-start.10 = (f32[1,132,2]{2,1,0:T(8,128)}, f32[1,132,2]{2,1,0:T(8,128)S(1)}, u32[]{:S(2)}, u32[]{:S(2)}) collective-permute-start(f32[1,132,2]{2,1,0:T(8,128)} %get-tuple-element.1499), channel_id=1, source_target_pairs={{1,0},{2,1},{3,2},{4,3},{5,4},{6,5},{7,6},{0,7},{9,8},{10,9},{11,1... | collective-permute-start | bytes 3176 | tf_op jit(solution)/shard_map/while/body/eval_jaxpr/ppermute | solution.py:22
  177.9 10.6 %collective-permute-start.11 = (f32[1,132,2]{2,1,0:T(8,128)S(1)}, f32[1,132,2]{2,1,0:T(8,128)S(1)}, u32[]{:S(2)}, u32[]{:S(2)}) collective-permute-start(f32[1,132,2]{2,1,0:T(8,128)S(1)} %get-tuple-element.1500), channel_id=1, source_target_pairs={{0,1},{1,2},{2,3},{3,4},{4,5},{5,6},{6,7},{7,0},{8,9},{9,10},{10,1... | collective-permute-start | bytes 3176 | tf_op jit(solution)/shard_map/while/body/eval_jaxpr/ppermute | solution.py:19
  226.1 4.5 collective-permute-start.13
  231.3 15.3 %collective-permute-start.14 = (f32[1,132,2]{2,1,0:T(8,128)}, f32[1,132,2]{2,1,0:T(8,128)}, u32[]{:S(2)}, u32[]{:S(2)}) collective-permute-start(f32[1,132,2]{2,1,0:T(8,128)} %get-tuple-element.1515), channel_id=1, source_target_pairs={{1,0},{2,1},{3,2},{4,3},{5,4},{6,5},{7,6},{0,7},{9,8},{10,9},{11,1... | collective-permute-start | bytes 3176 | tf_op jit(solution)/shard_map/while/body/eval_jaxpr/ppermute | solution.py:22
  233.4 13.2 %collective-permute-start.15 = (f32[1,132,2]{2,1,0:T(8,128)}, f32[1,132,2]{2,1,0:T(8,128)}, u32[]{:S(2)}, u32[]{:S(2)}) collective-permute-start(f32[1,132,2]{2,1,0:T(8,128)} %get-tuple-element.1516), channel_id=1, source_target_pairs={{0,1},{1,2},{2,3},{3,4},{4,5},{5,6},{6,7},{7,0},{8,9},{9,10},{10,1... | collective-permute-start | bytes 3176 | tf_op jit(solution)/shard_map/while/body/eval_jaxpr/ppermute | solution.py:19
  294.4 4.5 collective-permute-start.1
  299.0 23.0 %collective-permute-start.2 = (f32[1,132,2]{2,1,0:T(8,128)S(1)}, f32[1,132,2]{2,1,0:T(8,128)S(1)}, u32[]{:S(2)}, u32[]{:S(2)}) collective-permute-start(f32[1,132,2]{2,1,0:T(8,128)S(1)} %get-tuple-element.1460), channel_id=1, source_target_pairs={{1,0},{2,1},{3,2},{4,3},{5,4},{6,5},{7,6},{0,7},{9,8},{10,9},{11,1... | collective-permute-start | bytes 3176 | tf_op jit(solution)/shard_map/while/body/eval_jaxpr/ppermute | solution.py:22
  301.3 20.8 %collective-permute-start.3 = (f32[1,132,2]{2,1,0:T(8,128)S(1)}, f32[1,132,2]{2,1,0:T(8,128)S(1)}, u32[]{:S(2)}, u32[]{:S(2)}) collective-permute-start(f32[1,132,2]{2,1,0:T(8,128)S(1)} %get-tuple-element.1461), channel_id=1, source_target_pairs={{0,1},{1,2},{2,3},{3,4},{4,5},{5,6},{6,7},{7,0},{8,9},{9,10},{10,1... | collective-permute-start | bytes 3176 | tf_op jit(solution)/shard_map/while/body/eval_jaxpr/ppermute | solution.py:19
  353.9 4.5 collective-permute-start.5
  358.5 13.2 %collective-permute-start.6 = (f32[1,132,2]{2,1,0:T(8,128)S(1)}, f32[1,132,2]{2,1,0:T(8,128)S(1)}, u32[]{:S(2)}, u32[]{:S(2)}) collective-permute-start(f32[1,132,2]{2,1,0:T(8,128)S(1)} %get-tuple-element.1483), channel_id=1, source_target_pairs={{1,0},{2,1},{3,2},{4,3},{5,4},{6,5},{7,6},{0,7},{9,8},{10,9},{11,1... | collective-permute-start | bytes 3176 | tf_op jit(solution)/shard_map/while/body/eval_jaxpr/ppermute | solution.py:22
  360.7 11.0 %collective-permute-start.7 = (f32[1,132,2]{2,1,0:T(8,128)S(1)}, f32[1,132,2]{2,1,0:T(8,128)S(1)}, u32[]{:S(2)}, u32[]{:S(2)}) collective-permute-start(f32[1,132,2]{2,1,0:T(8,128)S(1)} %get-tuple-element.1484), channel_id=1, source_target_pairs={{0,1},{1,2},{2,3},{3,4},{4,5},{5,6},{6,7},{7,0},{8,9},{9,10},{10,1... | collective-permute-start | bytes 3176 | tf_op jit(solution)/shard_map/while/body/eval_jaxpr/ppermute | solution.py:19
  406.2 4.5 collective-permute-start.9
  411.3 12.5 %collective-permute-start.10 = (f32[1,132,2]{2,1,0:T(8,128)}, f32[1,132,2]{2,1,0:T(8,128)S(1)}, u32[]{:S(2)}, u32[]{:S(2)}) collective-permute-start(f32[1,132,2]{2,1,0:T(8,128)} %get-tuple-element.1499), channel_id=1, source_target_pairs={{1,0},{2,1},{3,2},{4,3},{5,4},{6,5},{7,6},{0,7},{9,8},{10,9},{11,1... | collective-permute-start | bytes 3176 | tf_op jit(solution)/shard_map/while/body/eval_jaxpr/ppermute | solution.py:22
  413.5 10.3 %collective-permute-start.11 = (f32[1,132,2]{2,1,0:T(8,128)S(1)}, f32[1,132,2]{2,1,0:T(8,128)S(1)}, u32[]{:S(2)}, u32[]{:S(2)}) collective-permute-start(f32[1,132,2]{2,1,0:T(8,128)S(1)} %get-tuple-element.1500), channel_id=1, source_target_pairs={{0,1},{1,2},{2,3},{3,4},{4,5},{5,6},{6,7},{7,0},{8,9},{9,10},{10,1... | collective-permute-start | bytes 3176 | tf_op jit(solution)/shard_map/while/body/eval_jaxpr/ppermute | solution.py:19
  461.4 4.5 collective-permute-start.13
  466.7 15.1 %collective-permute-start.14 = (f32[1,132,2]{2,1,0:T(8,128)}, f32[1,132,2]{2,1,0:T(8,128)}, u32[]{:S(2)}, u32[]{:S(2)}) collective-permute-start(f32[1,132,2]{2,1,0:T(8,128)} %get-tuple-element.1515), channel_id=1, source_target_pairs={{1,0},{2,1},{3,2},{4,3},{5,4},{6,5},{7,6},{0,7},{9,8},{10,9},{11,1... | collective-permute-start | bytes 3176 | tf_op jit(solution)/shard_map/while/body/eval_jaxpr/ppermute | solution.py:22
  468.8 13.0 %collective-permute-start.15 = (f32[1,132,2]{2,1,0:T(8,128)}, f32[1,132,2]{2,1,0:T(8,128)}, u32[]{:S(2)}, u32[]{:S(2)}) collective-permute-start(f32[1,132,2]{2,1,0:T(8,128)} %get-tuple-element.1516), channel_id=1, source_target_pairs={{0,1},{1,2},{2,3},{3,4},{4,5},{5,6},{6,7},{7,0},{8,9},{9,10},{10,1... | collective-permute-start | bytes 3176 | tf_op jit(solution)/shard_map/while/body/eval_jaxpr/ppermute | solution.py:19
  (115 other events, 2319.4 us)
